TPU v7x, 128 devices: a 2x2x16 block of a 8x8x16 slice. The times are simulated.
128 devices in a mesh: grp: 4 (over y, x), seq: 32 (over z, core).
Axes of the slice: x: 2, y: 2, z: 16, core: 2. Of those that a mesh axis runs over, the one named last changes fastest.
The devices are a block of a 8x8x16 slice.
Arguments:
- queries: bfloat16 [2048, 4096], P(('grp', 'seq')), parts along dimension 0, may hold values from -36 to 36
- new_keys: bfloat16 [2048, 1024], P(('grp', 'seq')), parts along dimension 0, may hold values from -24 to 24
- new_values: bfloat16 [2048, 1024], P(('grp', 'seq')), parts along dimension 0, may hold values from -12 to 12
- suffix_keys: bfloat16 [2048, 256, 1024], P(('grp', 'seq')), parts along dimension 0, may hold values from -18 to 18
- suffix_values: bfloat16 [2048, 256, 1024], P(('grp', 'seq')), parts along dimension 0, may hold values from -12 to 12
- suffix_lens: int32 [2048], P(('grp', 'seq')), parts along dimension 0, may hold values from 1 to 256, 65536 in all
- prefix_keys: bfloat16 [8192, 16, 1024], P(('grp', 'seq')), parts along dimension 0, may hold values from -12 to 12
- prefix_values: bfloat16 [8192, 16, 1024], P(('grp', 'seq')), parts along dimension 0, may hold values from -12 to 12
- page_table: int32 [8, 1024], P('grp'), parts along dimension 0, may hold values from 0 to 2047, as said below
- prefix_id: int32 [2048], P('grp'), parts along dimension 0, may hold values from 0 to 1
Outputs:
- attn_out: bfloat16 [2048, 4096], P(('grp', 'seq')), parts along dimension 0
There are 4 independent parts, one for each index of `grp`. A program takes and returns all parts, laid end to end along the dimension named above; each array names one. Nothing has to cross between parts.
Inputs may be any that keep to these rules, and one draw needn't show every extreme that they name: `page_table`: every page id 0 to 2047 stands exactly once in the table. Each run of 64 page ids that starts at a multiple of 64 holds at least one page of every prefix.
All inputs are finite; a program needn't handle non-finite values. No bound on the sum of `suffix_lens` on one device may be relied on, other than what follows from the above.
Results may differ from a plain program's by a relative error of at most 0.005.
Values may be sent and summed in bfloat16 or wider, within the bound.
No kernel may reach another device: no remote copies, remote signals or barrier semaphores. Data moves between devices by JAX's collectives and lax.ppermute only.
A program may use at most 192 MiB of HBM per device.

v0:
```python
import math
import jax
import jax.numpy as jnp
from jax import lax
from jax.sharding import Mesh
from jax.sharding import PartitionSpec as P

H = 32
KV = 8
HD = 128
NPREF = 2
SEQ = ("seq_0", "seq_1")
GRP_SEQ = ("grp", "seq_0", "seq_1")
floor_score = -1e30


def split_up(array, dim, peers):
    before, after = (array.shape[:dim], array.shape[dim + 1 :])
    return jnp.moveaxis(array.reshape(*before, peers, -1, *after), dim, 0)


def laid_out(tiles, dim):
    tiles = jnp.moveaxis(tiles, 0, dim)
    lengths = tiles.shape
    return tiles.reshape(*lengths[:dim], lengths[dim] * lengths[dim + 1], *lengths[dim + 2 :])


def moved_by_axis(tiles, axes, sequence):
    lengths = [lax.axis_size(a) for a in axes]
    tiles = tiles.reshape(*lengths, *tiles.shape[1:])
    for k in sequence:
        tiles = lax.all_to_all(tiles, axes[k], split_axis=k, concat_axis=k, tiled=True)
    return tiles.reshape(-1, *tiles.shape[len(axes) :])


def two_step_exchange(array, groups, sequence, split_dim, concat_dim):
    peers = lax.axis_size(groups[0]) * lax.axis_size(groups[1])
    tiles = split_up(array, split_dim, peers)
    return laid_out(moved_by_axis(tiles, groups, sequence), concat_dim)


def local(
    queries,
    new_keys,
    new_values,
    suffix_keys,
    suffix_values,
    suffix_lens,
    prefix_keys,
    prefix_values,
    page_table,
    prefix_id,
):
    local_rows = queries.shape[0]
    group_size = H // KV
    softmax_scale = 1.0 / math.sqrt(HD)
    owner_count = lax.axis_size(SEQ)
    owner_index = lax.axis_index(SEQ)
    pages_dev = prefix_keys.shape[0]
    local_ids = owner_index * pages_dev + jnp.arange(pages_dev, dtype=jnp.int32)
    page_hits = jnp.any(page_table[:, :, None] == local_ids[None, None, :], axis=1)
    page_label = jnp.sum(
        page_hits.astype(jnp.int32) * jnp.arange(NPREF, dtype=jnp.int32)[:, None], axis=0
    )
    token_label = jnp.repeat(page_label, prefix_keys.shape[1])
    keys_local = prefix_keys.reshape(-1, KV, HD)
    values_local = prefix_values.reshape(-1, KV, HD)
    shard_rows = lax.all_gather(queries, SEQ, axis=0, tiled=True)
    piece_rows = shard_rows.shape[0]
    query_head_count = shard_rows.reshape(piece_rows, KV, group_size, HD)
    scores = (
        jnp.einsum(
            "bkgd,tkd->bkgt", query_head_count, keys_local, preferred_element_type=jnp.float32
        )
        * softmax_scale
    )
    allowed = (prefix_id[:, None] == token_label[None, :])[:, None, None, :]
    scores = jnp.where(allowed, scores, floor_score)
    row_peak = jnp.max(scores, axis=3)
    weights = jnp.where(allowed, jnp.exp(scores - row_peak[..., None]), 0.0)
    weight_sum = jnp.sum(weights, axis=3)
    numerator = jnp.einsum(
        "bkgt,tkd->bkgd",
        weights.astype(jnp.bfloat16),
        values_local,
        preferred_element_type=jnp.float32,
    )
    piece_out = (numerator / weight_sum[..., None]).astype(jnp.bfloat16).reshape(piece_rows, -1)
    piece_lse = (row_peak + jnp.log(weight_sum)).reshape(-1)
    out_all = piece_out
    lse_all = piece_lse
    out_all, lse_all = (out_all, lse_all)
    resident_heads = queries.reshape(local_rows, KV, group_size, HD)
    slot_count = suffix_keys.shape[1]
    own_keys = suffix_keys.reshape(local_rows, slot_count, KV, HD)
    own_values = suffix_values.reshape(local_rows, slot_count, KV, HD)
    suffix_scores = (
        jnp.einsum("bkgd,btkd->bkgt", resident_heads, own_keys, preferred_element_type=jnp.float32)
        * softmax_scale
    )
    suffix_live = (jnp.arange(slot_count, dtype=jnp.int32)[None, :] < suffix_lens[:, None])[
        :, None, None, :
    ]
    suffix_scores = jnp.where(suffix_live, suffix_scores, floor_score)
    incoming_keys = new_keys.reshape(local_rows, KV, HD)
    incoming_values = new_values.reshape(local_rows, KV, HD)
    incoming_scores = (
        jnp.einsum(
            "iqnc,iqc->iqn", resident_heads, incoming_keys, preferred_element_type=jnp.float32
        )
        * softmax_scale
    )
    home_peak = jnp.maximum(jnp.max(suffix_scores, axis=3), incoming_scores)
    suffix_weights = jnp.where(suffix_live, jnp.exp(suffix_scores - home_peak[..., None]), 0.0)
    fresh_weights = jnp.exp(incoming_scores - home_peak)
    home_mass = jnp.sum(suffix_weights, axis=3) + fresh_weights
    resident_numerator = jnp.einsum(
        "bkgt,btkd->bkgd",
        suffix_weights.astype(jnp.bfloat16),
        own_values,
        preferred_element_type=jnp.float32,
    )
    resident_numerator = resident_numerator + jnp.einsum(
        "cqx,cqh->cqxh",
        fresh_weights.astype(jnp.bfloat16),
        incoming_values,
        preferred_element_type=jnp.float32,
    )
    home_out = (
        resident_numerator.reshape(local_rows, H, HD) / home_mass.reshape(local_rows, H)[..., None]
    )
    home_lse = (home_peak + jnp.log(home_mass)).reshape(local_rows, H)
    recv_out = lax.all_to_all(out_all, SEQ, split_axis=0, concat_axis=0, tiled=True)
    recv_lse = two_step_exchange(lse_all, ("seq_0", "seq_1"), (0, 1), 0, 0)
    recv_out = recv_out.reshape(owner_count, local_rows, H, HD).astype(jnp.float32)
    recv_lse = recv_lse.reshape(owner_count, local_rows, H)
    overall = jnp.maximum(jnp.max(recv_lse, axis=0), home_lse)
    factor = jnp.exp(recv_lse - overall[None])
    home_factor = jnp.exp(home_lse - overall)
    merged = jnp.sum(factor[..., None] * recv_out, axis=0) + home_factor[..., None] * home_out
    divisor = jnp.sum(factor, axis=0) + home_factor
    result = merged / divisor[..., None]
    return result.reshape(local_rows, H * HD).astype(jnp.bfloat16)


def solution(mesh):
    finer = Mesh(mesh.devices.reshape(mesh.shape["grp"], 16, 2), ("grp", "seq_0", "seq_1"))
    placed = (
        P(GRP_SEQ, None),
        P(GRP_SEQ, None),
        P(GRP_SEQ, None),
        P(GRP_SEQ, None, None),
        P(GRP_SEQ, None, None),
        P(GRP_SEQ),
        P(GRP_SEQ, None, None),
        P(GRP_SEQ, None, None),
        P("grp", None),
        P("grp"),
    )
    return jax.shard_map(
        local, mesh=finer, in_specs=placed, out_specs=P(GRP_SEQ, None), check_vma=False
    )
```

profile of v0, /device:TPU:196, one launch (start us, length us, event | category | flops | bytes accessed | tf_op | source)
XLA Modules:
  0.0 416.6 jit_solution(18046694975865880735)
XLA Ops:
  6.5 0.0 all-gather.2.cloned.1.call-start
  6.6 0.7 all-gather.2.cloned.1.call-update
  7.3 0.9 compare_reduce_fusion
  8.3 0.1 broadcast_in_dim.54
  8.3 0.1 eq.36
  8.4 2.2 copy.106
  10.6 3.6 copy.107
  14.2 0.0 copy-done.3
  14.2 0.4 broadcast_compare_fusion
  14.6 70.5 %all-gather.2.cloned.1.call-done = bf16[512,4096]{1,0:T(8,128)(2,1)} async-done(((bf16[16,4096]{1,0:T(8,128)(2,1)}), bf16[512,4096]{1,0:T(8,128)(2,1)}) %all-gather.2.cloned.1.call-update) | async-done | bytes 4194320 | tf_op jit(solution)/shard_map/all_gather | solution.py:68
  85.1 6.5 %copy.78 = bf16[512,4096]{0,1:T(8,128)(2,1)} copy(bf16[512,4096]{1,0:T(8,128)(2,1)} %all-gather.2.cloned.1.call-done) | data formatting | bytes 8388608 | tf_op jit(solution)/shard_map/all_gather | solution.py:68
  91.6 27.0 %fusion = (f32[512,8,4]{0,2,1:T(4,128)S(1)}, f32[8,1024,512,4]{2,1,3,0:T(8,128)}) fusion(pred[512,1024]{0,1:T(8,128)(4,1)S(1)} %broadcast_compare_fusion, bf16[512,8,4,128]{0,3,2,1:T(8,128)(2,1)} %bitcast.83, bf16[1024,8,128,1]{2,1,0,3:T(8,128)(2,1)S(1)} %bitcast.84), kind=kOutput, calls=%fused_computation.2 | convolution fusion | flops 4345282560 | bytes 73990144 | tf_op jit(solution)/shard_map/bkgd,tkd->bkgt/dot_general | solution.py:72
  118.6 21.8 %fusion.2 = f32[512,8,4]{0,2,1:T(4,128)S(1)} fusion(f32[8,1024,512,4]{2,1,3,0:T(8,128)} %get-tuple-element.13, f32[512,8,4]{0,2,1:T(4,128)S(1)} %get-tuple-element.12, pred[512,1024]{0,1:T(8,128)(4,1)S(1)} %broadcast_compare_fusion), kind=kLoop, calls=%fused_computation.4 | loop fusion | flops 83869696 | bytes 67764224 | tf_op jit(solution)/shard_map/reduce_sum | solution.py:81
  140.4 0.8 copy.81
  141.2 2.3 add.44
  143.5 8.4 %all-to-all-start = ((f32[16,2,512]{2,1,0:T(2,128)}), f32[16,2,512]{2,1,0:T(2,128)S(1)}, u32[]{:S(2)}, u32[]{:S(2)}) async-start(f32[16,2,512]{2,1,0:T(2,128)} %add.44), calls=%async_computation | async-start | bytes 131072 | tf_op jit(solution)/shard_map/all_to_all | solution.py:32
  151.9 29.9 %fusion.12 = bf16[512,8,4,128]{3,0,2,1:T(8,128)(2,1)} fusion(f32[512,8,4]{0,2,1:T(4,128)S(1)} %fusion.2, f32[8,1024,512,4]{2,1,3,0:T(8,128)} %get-tuple-element.13, f32[512,8,4]{0,2,1:T(4,128)S(1)} %get-tuple-element.12, pred[512,1024]{0,1:T(8,128)(4,1)S(1)} %broadcast_compare_fusion, bf16[1024,8,128,1]{2,1,0,3:T(8,128)(2,1)} %bitcast.87), kind=kOutput, calls=%fused_computation.14 | convolution fusion | flops 4383047680 | bytes 74055680 | tf_op jit(solution)/shard_map/bkgt,tkd->bkgd/dot_general | solution.py:82
  181.8 7.3 %copy.89 = bf16[512,8,4,128]{3,2,1,0:T(4,128)(2,1)} copy(bf16[512,8,4,128]{3,0,2,1:T(8,128)(2,1)} %fusion.12) | data formatting | bytes 8388608 | tf_op jit(solution)/shard_map/convert_element_type | solution.py:88
  189.2 7.8 %all_to_all.14 = bf16[32,16,4096]{2,1,0:T(8,128)(2,1)} reshape(bf16[512,8,4,128]{3,2,1,0:T(4,128)(2,1)} %copy.89) | data formatting | bytes 8388608 | tf_op jit(solution)/shard_map/all_to_all | solution.py:133
  197.0 0.0 all-to-all-done
  197.1 3.8 all_to_all.19
  200.9 12.6 %all-to-all-start.2 = ((bf16[32,16,4096]{2,1,0:T(8,128)(2,1)}), bf16[32,16,4096]{2,1,0:T(8,128)(2,1)}, u32[]{:S(2)}, u32[]{:S(2)}) async-start(bf16[32,16,4096]{2,1,0:T(8,128)(2,1)} %all_to_all.14), calls=%async_computation.2 | async-start | bytes 8388608 | tf_op jit(solution)/shard_map/all_to_all | solution.py:133
  213.4 0.1 reshape.158
  213.6 0.0 copy-done.4
  213.6 0.1 iota_compare_fusion
  213.7 0.3 fusion.44
  213.9 5.7 %fusion.43 = (f32[16,8,4]{2,1,0:T(8,128)S(1)}, f32[16,8,4,256]{3,2,1,0:T(4,128)S(1)}) fusion(bf16[16,8,4,128]{3,2,1,0:T(4,128)(2,1)S(1)} %reshape.158, pred[16,256]{1,0:T(8,128)(4,1)S(1)} %iota_compare_fusion, bf16[16,256,1024]{2,1,0:T(8,128)(2,1)} %param.13), kind=kOutput, calls=%fused_computation.53 | convolution fusion | flops 33947136 | bytes 9050112 | tf_op jit(solution)/shard_map/bkgd,btkd->bkgt/dot_general | solution.py:98
  219.7 0.4 fusion.28
  220.2 0.1 reshape.166
  220.3 0.1 copy.85
  220.4 0.0 copy-done.2
  220.5 0.1 copy.92
  220.6 0.1 copy.93
  220.7 4.7 %fusion.21 = f32[16,8,4,128]{3,2,1,0:T(4,128)S(1)} fusion(f32[16,8,4,256]{3,2,1,0:T(4,128)S(1)} %get-tuple-element.15, f32[16,8,4]{2,1,0:T(8,128)S(1)} %get-tuple-element.6, pred[16,256]{1,0:T(8,128)(4,1)S(1)} %iota_compare_fusion, f32[16,8,128]{2,1,0:T(8,128)S(1)} %bitcast.98, f32[16,8,4]{2,1,0:T(8,128)S(1)} %get-tuple-element.5, ...), kind=kOutput, calls=%fused_computation.20 | convolution fusion | flops 34078720 | bytes 9248768 | tf_op jit(solution)/shard_map/bkgt,btkd->bkgd/dot_general | solution.py:117
  225.3 0.1 reshape.165
  225.4 0.1 copy.86
  225.5 0.1 reduce_max.31
  225.6 0.1 reduce_sum.52
  225.7 0.1 copy.83
  225.8 0.1 reshape_reshape_reshape.4
  226.0 4.6 %mul.68 = f32[32,16,32,128]{3,2,1,0:T(8,128)} broadcast(f32[32,16,32]{2,1,0:T(8,128)S(1)} %subtract_exponential_fusion), dimensions={0,1,2} | broadcast | bytes 8454144 | tf_op jit(solution)/shard_map/mul | solution.py:140
  230.6 9.4 %mul.69 = f32[32,16,4096]{2,1,0:T(8,128)} reshape(f32[32,16,32,128]{3,2,1,0:T(8,128)} %mul.68) | data formatting | bytes 16777216 | tf_op jit(solution)/shard_map/mul | solution.py:140
  240.0 162.5 %all-to-all-done.2 = bf16[32,16,4096]{2,1,0:T(8,128)(2,1)} async-done(((bf16[32,16,4096]{2,1,0:T(8,128)(2,1)}), bf16[32,16,4096]{2,1,0:T(8,128)(2,1)}, u32[]{:S(2)}, u32[]{:S(2)}) %all-to-all-start.2) | async-done | bytes 4194336 | tf_op jit(solution)/shard_map/all_to_all | solution.py:133
  402.5 5.7 %multiply_reduce_fusion = f32[16,4096]{1,0:T(8,128)S(1)} fusion(f32[32,16,4096]{2,1,0:T(8,128)} %mul.69, bf16[32,16,4096]{2,1,0:T(8,128)(2,1)} %all-to-all-done.2), kind=kLoop, calls=%fused_computation.15 | loop fusion | flops 6225920 | bytes 12845056 | tf_op jit(solution)/shard_map/reduce_sum | solution.py:140
  408.2 0.1 div.35
  408.3 0.1 div.38
  408.5 0.1 mul.71
  408.6 1.1 fusion.30
  (21 shorter events, 0.3 us)
Async XLA Ops:
  6.5 7.7 %copy-start.3 = (s32[512]{0:T(512)S(1)}, s32[512]{0:T(512)}, u32[]{:S(2)}) copy-start(s32[512]{0:T(512)} %param.19) | copy-start | bytes 6148
  6.5 78.6 %all-gather.2.cloned.1.call-start = ((), (), s32[]{:S(2)}) async-start(), calls=%async_computation.3 | async-start | bytes 4325376 | tf_op jit(solution)/shard_map/all_gather | solution.py:68
  143.5 53.5 %all-to-all-start = ((f32[16,2,512]{2,1,0:T(2,128)}), f32[16,2,512]{2,1,0:T(2,128)S(1)}, u32[]{:S(2)}, u32[]{:S(2)}) async-start(f32[16,2,512]{2,1,0:T(2,128)} %add.44), calls=%async_computation | async-start | bytes 131072 | tf_op jit(solution)/shard_map/all_to_all | solution.py:32
  189.2 24.3 %copy-start = (bf16[16,4096]{1,0:T(8,128)(2,1)S(1)}, bf16[16,4096]{1,0:T(8,128)(2,1)}, u32[]{:S(2)}) copy-start(bf16[16,4096]{1,0:T(8,128)(2,1)} %param.10) | copy-start | bytes 393220
  189.2 24.3 %copy-start.1 = (bf16[16,1024]{1,0:T(8,128)(2,1)S(1)}, bf16[16,1024]{1,0:T(8,128)(2,1)}, u32[]{:S(2)}) copy-start(bf16[16,1024]{1,0:T(8,128)(2,1)} %param.11) | copy-start | bytes 98308
  189.2 24.4 %copy-start.4 = (s32[16]{0:T(128)S(1)}, s32[16]{0:T(128)}, u32[]{:S(2)}) copy-start(s32[16]{0:T(128)} %param.15) | copy-start | bytes 196
  200.9 19.6 %copy-start.2 = (bf16[16,1024]{1,0:T(8,128)(2,1)S(1)}, bf16[16,1024]{1,0:T(8,128)(2,1)}, u32[]{:S(2)}) copy-start(bf16[16,1024]{1,0:T(8,128)(2,1)} %param.12) | copy-start | bytes 98308
  200.9 201.7 %all-to-all-start.2 = ((bf16[32,16,4096]{2,1,0:T(8,128)(2,1)}), bf16[32,16,4096]{2,1,0:T(8,128)(2,1)}, u32[]{:S(2)}, u32[]{:S(2)}) async-start(bf16[32,16,4096]{2,1,0:T(8,128)(2,1)} %all_to_all.14), calls=%async_computation.2 | async-start | bytes 8388608 | tf_op jit(solution)/shard_map/all_to_all | solution.py:133
Sparse Core Ops, SparseCore 0:
  9.1 76.0 all-gather.1
where the time goes:
time: 418 us; the launch traced here: 417 us
  waiting for transfers between devices  234 us (56%)
  matrix products  67.5 us (16%)
  local copies, waits for them, and re-layouts  46.3 us (11%)
  other arithmetic  30.6 us (7%)
  starting transfers between devices  21 us (5%)
  between operations  13.7 us (3%)
    all_to_all x1, waiting for transfers between devices, local(): lax.all_to_all(out_all, SEQ, split_axis=0, concat_axis=0, tiled=True)  163 us
    all_gather x1, waiting for transfers between devices, local(): shard_rows = lax.all_gather(queries, SEQ, axis=0, tiled=True)  70.5 us
    dot_general x1, matrix products, local(): jnp.einsum('bkgt,tkd->bkgd', weights.astype(jnp.bfloat16), values_local,...  29.9 us
    dot_general x1, matrix products, local(): jnp.einsum('bkgd,tkd->bkgt', query_head_count, keys_local, preferred_elem...  27 us
    reduce_sum x1, other arithmetic, local(): weight_sum = jnp.sum(weights, axis=3)  21.8 us
    mul x2, local copies, waits for them, and re-layouts, local(): factor[..., None] * recv_out  14 us
    all_to_all x1, starting transfers between devices, local(): lax.all_to_all(out_all, SEQ, split_axis=0, concat_axis=0, tiled=True)  12.6 us
    all_to_all x1, starting transfers between devices, moved_by_axis(): lax.all_to_all(tiles, axes[k], split_axis=k, concat_axis=k, tiled=True)  8.39 us
  transfers between devices with their start and end apart: 3, of which 2 were waited for; matrix products, arithmetic and copies ran while one was open for 17% of the time, Pallas kernels for 0%

commit v1 on v0

--- a/solution.py
+++ b/solution.py
@@ -1,3 +1,4 @@
+import functools
 import math
 import jax
 import jax.numpy as jnp
@@ -12,6 +13,16 @@
 SEQ = ("seq_0", "seq_1")
 GRP_SEQ = ("grp", "seq_0", "seq_1")
 floor_score = -1e30
+
+
+def turn_plate(frame, link_axis):
+    b_now = lax.axis_size(link_axis)
+    kept_arr = jnp.stack(b_now * [frame], 0)
+    f_now = lax.all_to_all(kept_arr, link_axis, 0, 0)
+    return jnp.concatenate(f_now, 0)
+
+
+_match_stacks_all = functools.partial(turn_plate, link_axis=SEQ)
 
 
 def split_up(array, dim, peers):
@@ -65,7 +76,7 @@
     token_label = jnp.repeat(page_label, prefix_keys.shape[1])
     keys_local = prefix_keys.reshape(-1, KV, HD)
     values_local = prefix_values.reshape(-1, KV, HD)
-    shard_rows = lax.all_gather(queries, SEQ, axis=0, tiled=True)
+    shard_rows = _match_stacks_all(queries)
     piece_rows = shard_rows.shape[0]
     query_head_count = shard_rows.reshape(piece_rows, KV, group_size, HD)
     scores = (

time: 418 us -> 538 us (1.29)
  waiting for transfers between devices: 234 us -> 345 us
  between operations: 13.7 us -> 0.25 us
  starting transfers between devices: 21 us -> 34.3 us
  matrix products: 67.5 us -> 73 us
    all_to_all x0 -> x1, waiting for transfers between devices: none -> 182 us  [turn_plate(): f_now = lax.all_to_all(kept_arr, link_axis, 0, 0)]
    all_gather x1 -> x0, waiting for transfers between devices: 70.5 us -> none  [local(): shard_rows = lax.all_gather(queries, SEQ, axis=0, tiled=True)]
    all_to_all x0 -> x1, starting transfers between devices: none -> 17.1 us  [turn_plate(): f_now = lax.all_to_all(kept_arr, link_axis, 0, 0)]
    another operation x0 -> x2, local copies, waits for them, and re-layouts: none -> 11.2 us  [the longest x1 7.71 us: local(): query_head_count = shard_rows.reshape(piece_rows, KV, group_size, HD)]
    all_gather x1 -> x0, local copies, waits for them, and re-layouts: 6.54 us -> none  [local(): shard_rows = lax.all_gather(queries, SEQ, axis=0, tiled=True)]
    dot_general x1, matrix products: 27 us -> 32.4 us  [local(): jnp.einsum('bkgd,tkd->bkgt', query_head_count, keys_local, preferred_elem...]
  transfers between devices with their start and end apart: 3 -> 3, of which waited for: 2 -> 2; matrix products, arithmetic and copies ran while one was open for 17% -> 13% of each run, Pallas kernels for 0% -> 0%
where the time goes in v1:
time: 538 us; the launch traced here: 537 us
  waiting for transfers between devices  345 us (64%)
  matrix products  73 us (14%)
  local copies, waits for them, and re-layouts  50.9 us (9%)
  starting transfers between devices  34.3 us (6%)
  other arithmetic  30.1 us (6%)
    all_to_all x1, waiting for transfers between devices, turn_plate(): f_now = lax.all_to_all(kept_arr, link_axis, 0, 0)  182 us
    all_to_all x1, waiting for transfers between devices, local(): lax.all_to_all(out_all, SEQ, split_axis=0, concat_axis=0, tiled=True)  163 us
    dot_general x1, matrix products, local(): jnp.einsum('bkgd,tkd->bkgt', query_head_count, keys_local, preferred_elem...  32.4 us
    dot_general x1, matrix products, local(): jnp.einsum('bkgt,tkd->bkgd', weights.astype(jnp.bfloat16), values_local,...  29.9 us
    reduce_sum x1, other arithmetic, local(): weight_sum = jnp.sum(weights, axis=3)  21.9 us
    all_to_all x1, starting transfers between devices, turn_plate(): f_now = lax.all_to_all(kept_arr, link_axis, 0, 0)  17.1 us
    mul x2, local copies, waits for them, and re-layouts, local(): factor[..., None] * recv_out  14 us
    all_to_all x1, starting transfers between devices, local(): lax.all_to_all(out_all, SEQ, split_axis=0, concat_axis=0, tiled=True)  12.6 us
  transfers between devices with their start and end apart: 3, of which 2 were waited for; matrix products, arithmetic and copies ran while one was open for 13% of the time, Pallas kernels for 0%

profile of v1, /device:TPU:196, one launch (start us, length us, event | category | flops | bytes accessed | tf_op | source)
XLA Modules:
  0.0 537.3 jit_solution(11735924267567269058)
XLA Ops:
  0.0 3.5 stack.2
  3.5 17.1 %all-to-all-start = ((bf16[32,16,4096]{2,1,0:T(8,128)(2,1)}), bf16[32,16,4096]{2,1,0:T(8,128)(2,1)}, u32[]{:S(2)}, u32[]{:S(2)}) async-start(bf16[32,16,4096]{2,1,0:T(8,128)(2,1)} %stack.2), calls=%async_computation | async-start | bytes 8388608 | tf_op jit(solution)/shard_map/all_to_all | solution.py:21
  20.7 0.0 copy-done.5
  20.7 0.2 compare_reduce_fusion
  21.0 0.1 broadcast_in_dim.54
  21.0 0.1 eq.36
  21.1 0.0 copy-done
  21.1 2.0 copy.100
  23.1 3.7 copy.101
  26.9 0.4 broadcast_compare_fusion
  27.2 182.4 %all-to-all-done = bf16[32,16,4096]{2,1,0:T(8,128)(2,1)} async-done(((bf16[32,16,4096]{2,1,0:T(8,128)(2,1)}), bf16[32,16,4096]{2,1,0:T(8,128)(2,1)}, u32[]{:S(2)}, u32[]{:S(2)}) %all-to-all-start) | async-done | bytes 4194336 | tf_op jit(solution)/shard_map/all_to_all | solution.py:21
  209.6 7.7 %reshape_reshape.3 = bf16[512,8,4,128]{3,2,1,0:T(4,128)(2,1)} reshape(bf16[32,16,4096]{2,1,0:T(8,128)(2,1)} %all-to-all-done) | data formatting | bytes 8388608 | tf_op jit(solution)/shard_map/reshape;reshape | solution.py:81
  217.4 32.4 %fusion = (f32[512,8,4]{0,2,1:T(4,128)S(1)}, f32[8,1024,512,4]{2,1,3,0:T(8,128)}) fusion(pred[512,1024]{0,1:T(8,128)(4,1)S(1)} %broadcast_compare_fusion, bf16[512,8,4,128]{3,2,1,0:T(4,128)(2,1)} %reshape_reshape.3, bf16[1024,8,128,1]{2,1,0,3:T(8,128)(2,1)S(1)} %bitcast.84), kind=kOutput, calls=%fused_computation.2 | convolution fusion | flops 4345282560 | bytes 73990144 | tf_op jit(solution)/shard_map/bkgd,tkd->bkgt/dot_general | solution.py:83
  249.8 21.9 %fusion.2 = f32[512,8,4]{0,2,1:T(4,128)S(1)} fusion(f32[8,1024,512,4]{2,1,3,0:T(8,128)} %get-tuple-element.13, f32[512,8,4]{0,2,1:T(4,128)S(1)} %get-tuple-element.12, pred[512,1024]{0,1:T(8,128)(4,1)S(1)} %broadcast_compare_fusion), kind=kLoop, calls=%fused_computation.4 | loop fusion | flops 83869696 | bytes 67764224 | tf_op jit(solution)/shard_map/reduce_sum | solution.py:92
  271.8 0.8 copy.76
  272.6 2.3 add.44
  274.9 4.5 all-to-all-start.1
  279.4 29.9 %fusion.12 = bf16[512,8,4,128]{3,0,2,1:T(8,128)(2,1)} fusion(f32[512,8,4]{0,2,1:T(4,128)S(1)} %fusion.2, f32[8,1024,512,4]{2,1,3,0:T(8,128)} %get-tuple-element.13, f32[512,8,4]{0,2,1:T(4,128)S(1)} %get-tuple-element.12, pred[512,1024]{0,1:T(8,128)(4,1)S(1)} %broadcast_compare_fusion, bf16[1024,8,128,1]{2,1,0,3:T(8,128)(2,1)} %bitcast.83), kind=kOutput, calls=%fused_computation.14 | convolution fusion | flops 4383047680 | bytes 74055680 | tf_op jit(solution)/shard_map/bkgt,tkd->bkgd/dot_general | solution.py:93
  309.4 7.3 %copy.84 = bf16[512,8,4,128]{3,2,1,0:T(4,128)(2,1)} copy(bf16[512,8,4,128]{3,0,2,1:T(8,128)(2,1)} %fusion.12) | data formatting | bytes 8388608 | tf_op jit(solution)/shard_map/convert_element_type | solution.py:99
  316.7 7.8 %all_to_all.18 = bf16[32,16,4096]{2,1,0:T(8,128)(2,1)} reshape(bf16[512,8,4,128]{3,2,1,0:T(4,128)(2,1)} %copy.84) | data formatting | bytes 8388608 | tf_op jit(solution)/shard_map/all_to_all | solution.py:144
  324.5 0.0 all-to-all-done.1
  324.6 3.8 all_to_all.24
  328.4 12.6 %all-to-all-start.3 = ((bf16[32,16,4096]{2,1,0:T(8,128)(2,1)}), bf16[32,16,4096]{2,1,0:T(8,128)(2,1)}, u32[]{:S(2)}, u32[]{:S(2)}) async-start(bf16[32,16,4096]{2,1,0:T(8,128)(2,1)} %all_to_all.18), calls=%async_computation.3 | async-start | bytes 8388608 | tf_op jit(solution)/shard_map/all_to_all | solution.py:144
  341.0 0.1 reshape.156
  341.0 0.0 copy-done.3
  341.1 0.1 iota_compare_fusion
  341.2 0.3 fusion.45
  341.5 5.7 %fusion.44 = (f32[16,8,4]{2,1,0:T(8,128)S(1)}, f32[16,8,4,256]{3,2,1,0:T(4,128)S(1)}) fusion(bf16[16,8,4,128]{3,2,1,0:T(4,128)(2,1)S(1)} %reshape.156, pred[16,256]{1,0:T(8,128)(4,1)S(1)} %iota_compare_fusion, bf16[16,256,1024]{2,1,0:T(8,128)(2,1)} %param.13), kind=kOutput, calls=%fused_computation.54 | convolution fusion | flops 33947136 | bytes 9050112 | tf_op jit(solution)/shard_map/bkgd,btkd->bkgt/dot_general | solution.py:109
  347.2 0.4 fusion.29
  347.7 0.1 reshape.164
  347.8 0.1 copy.80
  348.0 0.1 copy.87
  348.1 0.1 copy.88
  348.2 4.7 fusion.22
  352.8 0.1 reshape.163
  353.0 0.1 copy.81
  353.0 0.1 reduce_max.31
  353.2 0.1 reduce_sum.52
  353.2 0.1 copy.78
  353.3 0.1 reshape_reshape_reshape.4
  353.5 4.6 mul.68
  358.1 9.4 %mul.69 = f32[32,16,4096]{2,1,0:T(8,128)} reshape(f32[32,16,32,128]{3,2,1,0:T(8,128)} %mul.68) | data formatting | bytes 16777216 | tf_op jit(solution)/shard_map/mul | solution.py:151
  367.5 162.5 %all-to-all-done.3 = bf16[32,16,4096]{2,1,0:T(8,128)(2,1)} async-done(((bf16[32,16,4096]{2,1,0:T(8,128)(2,1)}), bf16[32,16,4096]{2,1,0:T(8,128)(2,1)}, u32[]{:S(2)}, u32[]{:S(2)}) %all-to-all-start.3) | async-done | bytes 4194336 | tf_op jit(solution)/shard_map/all_to_all | solution.py:144
  530.0 5.7 %multiply_reduce_fusion = f32[16,4096]{1,0:T(8,128)S(1)} fusion(f32[32,16,4096]{2,1,0:T(8,128)} %mul.69, bf16[32,16,4096]{2,1,0:T(8,128)(2,1)} %all-to-all-done.3), kind=kLoop, calls=%fused_computation.15 | loop fusion | flops 6225920 | bytes 12845056 | tf_op jit(solution)/shard_map/reduce_sum | solution.py:151
  535.7 0.1 div.35
  535.9 0.1 div.38
  536.0 0.1 mul.71
  536.1 1.1 fusion.31
  (27 shorter events, 0.3 us)
Async XLA Ops:
  0.0 20.7 %copy-start.5 = (s32[2,1024]{1,0:T(2,128)S(1)}, s32[2,1024]{1,0:T(2,128)}, u32[]{:S(2)}) copy-start(s32[2,1024]{1,0:T(2,128)} %param.18) | copy-start | bytes 24580
  0.0 21.1 %copy-start = (bf16[64,16,1024]{2,1,0:T(8,128)(2,1)S(1)}, bf16[64,16,1024]{2,1,0:T(8,128)(2,1)}, u32[]{:S(2)}) copy-start(bf16[64,16,1024]{2,1,0:T(8,128)(2,1)} %param.16) | copy-start | bytes 6291460
  3.5 23.3 %copy-start.6 = (s32[512]{0:T(512)S(1)}, s32[512]{0:T(512)}, u32[]{:S(2)}) copy-start(s32[512]{0:T(512)} %param.19) | copy-start | bytes 6148
  3.5 206.1 %all-to-all-start = ((bf16[32,16,4096]{2,1,0:T(8,128)(2,1)}), bf16[32,16,4096]{2,1,0:T(8,128)(2,1)}, u32[]{:S(2)}, u32[]{:S(2)}) async-start(bf16[32,16,4096]{2,1,0:T(8,128)(2,1)} %stack.2), calls=%async_computation | async-start | bytes 8388608 | tf_op jit(solution)/shard_map/all_to_all | solution.py:21
  23.1 194.2 %copy-start.1 = (bf16[128,8,8,128]{3,2,1,0:T(8,128)(2,1)S(1)}, bf16[128,8,8,128]{3,2,1,0:T(8,128)(2,1)}, u32[]{:S(2)}) copy-start(bf16[128,8,8,128]{3,2,1,0:T(8,128)(2,1)} %copy.100) | copy-start | bytes 6291460
  274.9 49.7 %all-to-all-start.1 = ((f32[16,2,512]{2,1,0:T(2,128)}), f32[16,2,512]{2,1,0:T(2,128)S(1)}, u32[]{:S(2)}, u32[]{:S(2)}) async-start(f32[16,2,512]{2,1,0:T(2,128)} %add.44), calls=%async_computation.1 | async-start | bytes 131072 | tf_op jit(solution)/shard_map/all_to_all | solution.py:43
  316.7 24.3 %copy-start.2 = (bf16[16,4096]{1,0:T(8,128)(2,1)S(1)}, bf16[16,4096]{1,0:T(8,128)(2,1)}, u32[]{:S(2)}) copy-start(bf16[16,4096]{1,0:T(8,128)(2,1)} %param.10) | copy-start | bytes 393220
  316.7 24.3 %copy-start.3 = (bf16[16,1024]{1,0:T(8,128)(2,1)S(1)}, bf16[16,1024]{1,0:T(8,128)(2,1)}, u32[]{:S(2)}) copy-start(bf16[16,1024]{1,0:T(8,128)(2,1)} %param.11) | copy-start | bytes 98308
  316.7 24.4 %copy-start.7 = (s32[16]{0:T(128)S(1)}, s32[16]{0:T(128)}, u32[]{:S(2)}) copy-start(s32[16]{0:T(128)} %param.15) | copy-start | bytes 196
  328.4 19.6 %copy-start.4 = (bf16[16,1024]{1,0:T(8,128)(2,1)S(1)}, bf16[16,1024]{1,0:T(8,128)(2,1)}, u32[]{:S(2)}) copy-start(bf16[16,1024]{1,0:T(8,128)(2,1)} %param.12) | copy-start | bytes 98308
  328.4 201.7 %all-to-all-start.3 = ((bf16[32,16,4096]{2,1,0:T(8,128)(2,1)}), bf16[32,16,4096]{2,1,0:T(8,128)(2,1)}, u32[]{:S(2)}, u32[]{:S(2)}) async-start(bf16[32,16,4096]{2,1,0:T(8,128)(2,1)} %all_to_all.18), calls=%async_computation.3 | async-start | bytes 8388608 | tf_op jit(solution)/shard_map/all_to_all | solution.py:144
